TPU v7x, 64 devices: a 2x2x8 block of a 4x4x8 slice. The times are simulated.
64 devices in a mesh: data: 4 (over x, y), expert: 16 (over z, core).
Axes of the slice: x: 2, y: 2, z: 8, core: 2. Of those that a mesh axis runs over, the one named last changes fastest.
The devices are a block of a 4x4x8 slice.
Arguments:
- x: bfloat16 [4096, 2048], P(('data', 'expert')), parts along dimension 0
- idx: int32 [4096, 6], P(('data', 'expert')), parts along dimension 0
- g: float32 [4096, 6], P(('data', 'expert')), parts along dimension 0
- hot_tok: int32 [2048], P(('data', 'expert')), parts along dimension 0
- W1: bfloat16 [64, 2048, 1408], P('expert')
- W3: bfloat16 [64, 2048, 1408], P('expert')
- W2: bfloat16 [64, 1408, 2048], P('expert')
Outputs:
- output: bfloat16 [4096, 2048], P(('data', 'expert')), parts along dimension 0
There are 4 independent parts. A program takes and returns all parts, laid end to end along the dimension named above; an argument that names none is the same for every part.
All inputs are finite; a program needn't handle non-finite values.
Results may differ from a plain program's by a relative error of at most 0.001.
Values are sent between devices in bfloat16 or wider.
A program may use at most 768 MiB of HBM per device.

v0:
```python
import functools

import jax
import jax.numpy as jnp
from jax import lax
from jax.experimental import pallas as pl
from jax.experimental.pallas import tpu as pltpu
from jax.sharding import PartitionSpec as P

F32 = jnp.float32
BF16 = jnp.bfloat16
RS_LAGS = (3, 5, 8, 11)
NP = 2


def _split3(v):
    hi = v.astype(BF16)
    r = v - hi.astype(F32)
    mid = r.astype(BF16)
    lo = (r - mid.astype(F32)).astype(BF16)
    return hi, mid, lo


def _kernel(cfg, x_ref, meta_ref, w1_ref, w3_ref, w2_ref, y_ref, xg, mg, w13, w2b, xs, u, hc, hh, pc, ph, qq, st, part, d2d, ring,
            x_sem, m_sem, w13_sem, w2_sem, ag_send, ag_recv, agd_recv, mg_send, mg_recv, mgd_recv, rs_send, rs_recv, rd_send, rd_recv):
    n, t, el, ch, cap, nc, nj, d_model, ff = cfg
    nz = n // 2
    half = nz // 2
    near = nz - half + 1
    blk = d_model // NP
    rc = 2 * cap
    rh = 2 * ch
    tt = 2 * t
    fcut = ff - ff % 256
    split = 2 * ff - fcut

    me = lax.axis_index('expert')
    z = me // 2
    c = me % 2
    right = ((z + 1) % nz) * 2 + c
    left = ((z + nz - 1) % nz) * 2 + c
    partner = z * 2 + (1 - c)
    nxt = (right, left)
    hot = me == 0
    cold = jnp.logical_not(hot)

    def remote(src, dst, ssem, rsem, dev):
        return pltpu.make_async_remote_copy(src_ref=src, dst_ref=dst, send_sem=ssem, recv_sem=rsem, device_id={'expert': dev},
                                            device_id_type=pl.DeviceIdType.MESH)

    def place(s, d):
        return 0 if s == 0 else nz - 1 if s == half else 2 * s - 1 if d == 0 else 2 * s

    def base(l):
        return 0 if l == 0 else nz * rh + (l - 1) * nz * rc

    def hops(k, d):
        return half - k % 2 if d == 0 else half - 1 + k % 2

    def w13_copies(e, slot):
        dst = w13.at[slot]
        sem = w13_sem.at[slot]
        out = [pltpu.make_async_copy(w1_ref.at[e], dst.at[:, pl.ds(0, ff)], sem)]
        if fcut < ff:
            out.append(pltpu.make_async_copy(w3_ref.at[e, :, pl.ds(fcut, ff - fcut)], dst.at[:, pl.ds(ff, ff - fcut)], sem))
        out.append(pltpu.make_async_copy(w3_ref.at[e, :, pl.ds(0, fcut)], dst.at[:, pl.ds(split, fcut)], sem))
        return out

    def w2_copies(j, slot):
        cols = pl.ds(pl.multiple_of(j * nc, nc), nc)
        return [pltpu.make_async_copy(w2_ref.at[l, :, cols], w2b.at[slot, l], w2_sem.at[slot]) for l in range(el)]

    def begin(copies):
        for cp in copies:
            cp.start()

    def done(copies):
        for cp in copies:
            cp.wait()

    x_copies = [pltpu.make_async_copy(x_ref.at[:, pl.ds(p * blk, blk)], xg.at[0, p, c], x_sem.at[p]) for p in range(NP)]
    m_copy = pltpu.make_async_copy(meta_ref, mg.at[0, c], m_sem)
    m_copy.start()
    begin(x_copies)
    for i in range(el - 1):
        begin(w13_copies(i + 1, i))
    for j in range(2):
        begin(w2_copies(j, j))

    barrier = pltpu.get_barrier_semaphore()
    for dev in (right, left, partner):
        pl.semaphore_signal(barrier, inc=1, device_id={'expert': dev}, device_id_type=pl.DeviceIdType.MESH)
    pl.semaphore_wait(barrier, 3)

    def share(q, p):
        src = xg.at[q, p, c]
        remote(src, src, ag_send, agd_recv.at[q, p], partner).start()

    def travels(s, d, p):
        return s < half or p == d

    def send(s, p):
        for d in range(2):
            if s <= half and travels(s, d, p):
                remote(xg.at[place(s - 1, d), p, c], xg.at[place(s, d), p, c], ag_send, ag_recv.at[d, s - 1, p], nxt[d]).start()

    def take(s, p):
        for d in range(2):
            if travels(s, d, p):
                dst = xg.at[place(s, d), p, c]
                remote(dst, dst, ag_send, ag_recv.at[d, s - 1, p], nxt[d]).wait_recv()
                if s < half and travels(s + 1, d, p):
                    remote(dst, xg.at[place(s + 1, d), p, c], ag_send, ag_recv.at[d, s, p], nxt[d]).start()
                share(place(s, d), p)

    def meta_send(s):
        for d in range(2):
            if s < half or (s == half and d == 0):
                remote(mg.at[place(s - 1, d), c], mg.at[place(s, d), c], mg_send, mg_recv.at[d, s - 1], nxt[d]).start()

    def meta_take(s):
        for d in range(2):
            if s < half or d == 0:
                dst = mg.at[place(s, d), c]
                remote(dst, dst, mg_send, mg_recv.at[d, s - 1], nxt[d]).wait_recv()
        meta_send(s + 1)
        for d in range(2):
            if s < half or d == 0:
                dst = mg.at[place(s, d), c]
                remote(dst, dst, mg_send, mgd_recv, partner).start()

    m_copy.wait()
    meta_send(1)
    remote(mg.at[0, c], mg.at[0, c], mg_send, mgd_recv, partner).start()
    x_copies[0].wait()
    send(1, 0)
    x_copies[1].wait()
    share(0, 0)
    share(0, 1)
    hc[...] = jnp.zeros(hc.shape, BF16)
    meta_take(1)
    send(1, 1)
    meta_take(2)
    take(1, 0)
    meta_take(3)
    take(1, 1)
    meta_take(4)

    def build():
        remote(mg.at[:, 0], mg.at[:, 0], mg_send, mgd_recv, partner).wait_recv()
        lane1 = lax.broadcasted_iota(jnp.int32, (8, tt), 1)
        s_i = lax.broadcasted_iota(jnp.int32, (tt, tt), 0)
        t_i = lax.broadcasted_iota(jnp.int32, (tt, tt), 1)
        upper = jnp.where((s_i < t_i) & (s_i // t == t_i // t), 1.0, 0.0).astype(BF16)
        core = (lax.broadcasted_iota(jnp.int32, (1, tt), 1) // t).astype(F32)
        row_c = lax.broadcasted_iota(jnp.int32, (el * rc, tt), 0).astype(F32)
        row_h = lax.broadcasted_iota(jnp.int32, (rh, tt), 0).astype(F32)
        col_c = lax.broadcasted_iota(jnp.int32, (tt, el * rc), 1).astype(F32)
        col_h = lax.broadcasted_iota(jnp.int32, (tt, rh), 1).astype(F32)
        far = jnp.full((1, tt), -4096.0, F32)

        def stats(q, carry):
            a = mg[q, 0]
            b = mg[q, 1]
            ids = jnp.where(lane1 < t, a, pltpu.roll(b, t, 1))
            gs = jnp.where(lane1 < t, pltpu.roll(a, t, 1), b)
            hits = [ids == (me * el + l).astype(F32) for l in range(el)]
            masks = [jnp.max(jnp.where(hit, 1.0, 0.0), axis=0, keepdims=True) for hit in hits]
            gates = [jnp.sum(jnp.where(hit, gs, 0.0), axis=0, keepdims=True) for hit in hits]
            st[0, q] = jnp.concatenate(masks + gates, axis=0)
            return carry

        lax.fori_loop(0, nz, stats, 0)
        every = st[0].reshape(nz * 2 * el, tt)
        st[1] = jnp.dot(every.astype(BF16), upper, preferred_element_type=F32).reshape(nz, 2 * el, tt)

        def fill(q, carry):
            mask = st[0, q]
            rank = st[1, q]
            codes = [jnp.where(mask[l:l + 1] > 0.0, core * cap + rank[l:l + 1] + float(l * rc), far) for l in range(el)]
            code_h = jnp.where(hot & (mask[0:1] > 0.0), core * ch + rank[0:1], far)
            codes[0] = jnp.where(hot, far, codes[0])
            rows = jnp.where(row_c == codes[0], 1.0, 0.0)
            for l in range(1, el):
                rows = jnp.where(row_c == codes[l], 1.0, rows)
            pc[q] = rows.astype(BF16)
            ph[q] = jnp.where(row_h == code_h, 1.0, 0.0).astype(BF16)
            cols = jnp.concatenate(codes + [mask[el:2 * el], code_h, jnp.zeros((128 - 2 * el - 1, tt), F32)], axis=0).T
            g = jnp.where(col_c == cols[:, 0:1], cols[:, el:el + 1], 0.0)
            for l in range(1, el):
                g = jnp.where(col_c == cols[:, l:l + 1], cols[:, el + l:el + l + 1], g)
            for p, piece in enumerate(_split3(g)):
                qq[q, :, p * el * rc:(p + 1) * el * rc] = piece
            g = jnp.where(col_h == cols[:, 2 * el:2 * el + 1], cols[:, el:el + 1], 0.0)
            qq[q, :, 3 * el * rc:] = jnp.concatenate(list(_split3(g)), axis=1)
            return carry

        lax.fori_loop(0, nz, fill, 0)

    build()
    take(2, 0)
    take(2, 1)

    def dispatch(first, count, is_hot):
        start = count * rh
        for i in range(count):
            q = first + i
            for p in range(NP):
                cols = slice(p * blk, (p + 1) * blk)
                xt = xg[q, p].reshape(tt, blk)
                res = jnp.dot(pc[q], xt, preferred_element_type=F32).astype(BF16)
                for l in range(1 if is_hot else 0, el):
                    row = (0 if l == 0 else start + (l - 1) * count * rc) + i * rc
                    xs[row:row + rc, cols] = res[l * rc:(l + 1) * rc]
                if is_hot:
                    xs[i * rh:(i + 1) * rh, cols] = jnp.dot(ph[q], xt, preferred_element_type=F32).astype(BF16)

    def products(xrow, urow, rows, slot):
        view = xs.at[pl.ds(xrow, rows)]
        out = pl.ds(urow, rows)

        def put(a, b, at):
            u[out, at] = (jax.nn.silu(a) * b).astype(BF16)

        for f in range(0, fcut, 256):
            put(jnp.dot(view[...], w13[slot, :, f:f + 256], preferred_element_type=F32),
                jnp.dot(view[...], w13[slot, :, split + f:split + f + 256], preferred_element_type=F32), slice(f, f + 256))
        if fcut < ff:
            ab = jnp.dot(view[...], w13[slot, :, fcut:split], preferred_element_type=F32)
            put(ab[:, :ff - fcut], ab[:, ff - fcut:], slice(fcut, ff))

    def one_pass(e, slot, first, count):
        @pl.when(hot & (e == 0))
        def _():
            products(0, first * rh, count * rh, slot)

        @pl.when(cold | (e > 0))
        def _():
            xrow = jnp.where(e == 0, 0, count * rh + (e - 1) * (count * rc))
            urow = jnp.where(e == 0, 0, nz * rh + (e - 1) * (nz * rc)) + first * rc
            products(pl.multiple_of(xrow, rc), pl.multiple_of(urow, rc), count * rc, slot)

    def gather_rows(first, count):
        for q in range(first, first + count):
            for p in range(NP):
                src = xg.at[q, p, 1 - c]
                remote(src, src, ag_send, agd_recv.at[q, p], partner).wait_recv()
        for is_hot, which in ((True, hot), (False, cold)):
            @pl.when(which)
            def _():
                dispatch(first, count, is_hot)

    gather_rows(0, near)

    def near_pass(i, carry):
        e = (i + 1) % el
        slot = i % (el - 1)
        done(w13_copies(e, slot))
        one_pass(e, slot, 0, near)

        @pl.when(i == 0)
        def _():
            begin(w13_copies(0, 0))
            take(3, 0)

        @pl.when(i == 1)
        def _():
            take(3, 1)

        return carry

    lax.fori_loop(0, el, near_pass, 0)
    take(4, 0)
    take(4, 1)
    gather_rows(near, nz - near)

    def far_pass(i, carry):
        e = (el - i) % el
        slot = (el - 1 - i) % (el - 1)

        @pl.when(i == el - 1)
        def _():
            done(w13_copies(1, 0))

        one_pass(e, slot, near, nz - near)

        @pl.when(i == 0)
        def _():
            begin(w13_copies(1, 0))

        return carry

    lax.fori_loop(0, el, far_pass, 0)

    def n_compute(j, slot, buf, is_hot):
        for l in range(el):
            big = is_hot and l == 0
            step = rh if big else rc
            h = jnp.dot(u[base(l):base(l) + nz * step, :], w2b[slot, l], preferred_element_type=F32).astype(BF16)
            for q in range(nz):
                if big:
                    hh[q] = h[q * rh:(q + 1) * rh]
                else:
                    hc[q, l * rc:(l + 1) * rc, :] = h[q * rc:(q + 1) * rc]
        for q in range(nz):
            if is_hot:
                tot = jnp.dot(qq[q], jnp.concatenate([hc[q]] * 3 + [hh[q]] * 3, axis=0), preferred_element_type=F32)
            else:
                tot = jnp.dot(qq[q, :, :3 * el * rc], jnp.concatenate([hc[q]] * 3, axis=0), preferred_element_type=F32)
            part[buf, q] = tot.reshape(2, t, nc)

    def d2d_copy(j, buf):
        return remote(part.at[buf, :, 1 - c], d2d.at[j], rd_send.at[buf], rd_recv.at[j], partner)

    def slot_of(s, d):
        return s - 1 if d == 0 else nz - 1 - s

    def rs_start(j):
        buf = j % 2
        d2d_copy(j, buf).wait_recv()
        for d in range(nz):
            d2d[j, d] += part[buf, d, c]
        for d in range(2):
            h = hops(j, d)
            dest = h + half - 1 if d == 0 else 2 * h - 1
            remote(d2d.at[j, dest], ring.at[j, slot_of(1, d)], rs_send, rs_recv.at[j, d, 0], nxt[d]).start()

    def rs_event(j, s, d):
        h = hops(j, d)
        dest = 2 * (h - s) if d == 0 else 2 * (h - s) - 1
        at = slot_of(s, d)
        here = ring.at[j, at]
        remote(here, here, rs_send, rs_recv.at[j, d, s - 1], nxt[d]).wait_recv()

        @pl.when(s < h)
        def _():
            ring[j, at] += d2d[j, dest]
            remote(here, ring.at[j, slot_of(s % half + 1, d)], rs_send, rs_recv.at[j, d, s % half], nxt[d]).start()

        @pl.when(s == h)
        def _():
            d2d[j, 0] += ring[j, at]

    def rs_round(r, carry):
        @pl.when(r < nj)
        def _():
            slot = r % 2
            for cp in w2_copies(r, slot):
                cp.wait()

            @pl.when(r >= 2)
            def _():
                d2d_copy(r - 2, slot).wait_send()

            @pl.when(hot)
            def _():
                n_compute(r, slot, slot, True)

            @pl.when(jnp.logical_not(hot))
            def _():
                n_compute(r, slot, slot, False)

            d2d_copy(r, slot).start()

            @pl.when(r + 2 < nj)
            def _():
                for cp in w2_copies(r + 2, slot):
                    cp.start()

        @pl.when((r >= 1) & (r - 1 < nj))
        def _():
            rs_start(r - 1)

        for s in range(1, half + 1):
            j = r - RS_LAGS[s - 1]
            for d in range(2):
                @pl.when((j >= 0) & (j < nj) & (s <= hops(j, d)))
                def _():
                    rs_event(j, s, d)

        j = r - RS_LAGS[half - 1]

        @pl.when((j >= 0) & (j < nj))
        def _():
            y_ref[:, pl.ds(pl.multiple_of(j * nc, nc), nc)] = d2d[j, 0].astype(BF16)

        return carry

    lax.fori_loop(0, nj + RS_LAGS[half - 1], rs_round, 0)

    for j in range(max(nj - 2, 0), nj):
        d2d_copy(j, j % 2).wait_send()
    for buf, sem in ((mg, mg_send), (xg, ag_send)):
        for view in (buf.at[pl.ds(0, nz - 1)], buf.at[nz - 1, 0]):
            remote(view, view, sem, mgd_recv, partner).wait_send()
    for j in range(nj):
        blk = ring.at[j]
        remote(blk, blk, rs_send, rs_recv.at[j, 0, 0], partner).wait_send()


def solution(mesh):
    n = mesh.shape['expert']

    def local(x, idx, g, hot_tok, w1, w3, w2):
        t, d = x.shape
        k = idx.shape[1]
        el, _, ff = w1.shape
        e = el * n
        ch = hot_tok.shape[0]
        need = 2 * ((t * k - ch + e - 2) // (e - 1))
        cap = -(-need // 16) * 16
        nc = 256
        nj = d // nc
        nz = n // 2
        near = nz - nz // 2 + 1
        rows = nz * 2 * (ch + (el - 1) * cap)
        xrows = near * 2 * (ch + (el - 1) * cap)
        ids = jnp.pad(idx.T.astype(F32), ((0, 8 - k), (0, 0)), constant_values=-1.0)
        meta = jnp.concatenate([ids, jnp.pad(g.T, ((0, 8 - k), (0, 0)))], axis=1)
        cfg = (n, t, el, ch, cap, nc, nj, d, ff)
        dma = pltpu.SemaphoreType.DMA
        return pl.pallas_call(
            functools.partial(_kernel, cfg),
            name='moe',
            out_shape=jax.ShapeDtypeStruct((t, d), BF16),
            in_specs=[pl.BlockSpec(memory_space=pl.ANY)] * 5,
            out_specs=pl.BlockSpec(memory_space=pltpu.VMEM),
            scratch_shapes=[
                pltpu.VMEM((nz, NP, 2, t, d // NP), BF16),
                pltpu.VMEM((nz, 2, 8, 2 * t), F32),
                pltpu.VMEM((el - 1, d, 2 * ff), BF16),
                pltpu.VMEM((2, el, ff, nc), BF16),
                pltpu.VMEM((xrows, d), BF16),
                pltpu.VMEM((rows, ff), BF16),
                pltpu.VMEM((nz, el * 2 * cap, nc), BF16),
                pltpu.VMEM((nz, 2 * ch, nc), BF16),
                pltpu.VMEM((nz, el * 2 * cap, 2 * t), BF16),
                pltpu.VMEM((nz, 2 * ch, 2 * t), BF16),
                pltpu.VMEM((nz, 2 * t, 6 * (el * cap + ch)), BF16),
                pltpu.VMEM((2, nz, 2 * el, 2 * t), F32),
                pltpu.VMEM((2, nz, 2, t, nc), F32),
                pltpu.VMEM((nj, nz, t, nc), F32),
                pltpu.VMEM((nj, nz - 1, t, nc), F32),
                dma((NP,)), dma(()), dma((el - 1,)), dma((2,)),
                dma(()), dma((2, nz // 2, NP)), dma((nz, NP)),
                dma(()), dma((2, nz // 2)), dma(()),
                dma(()), dma((nj, 2, nz // 2)), dma((2,)), dma((nj,)),
            ],
            compiler_params=pltpu.CompilerParams(collective_id=0, has_side_effects=True, vmem_limit_bytes=67043328),
        )(x, meta, w1, w3, w2)

    rows = P(('data', 'expert'))
    wspec = P('expert')
    return jax.shard_map(local, mesh=mesh, in_specs=(rows, rows, rows, rows, wspec, wspec, wspec), out_specs=rows, check_vma=False)
```

profile of v0, /device:TPU:30, one launch (start us, length us, event | category | flops | bytes accessed | tf_op | source)
XLA Modules:
  0.0 110.5 jit_solution(4584704613253159061)
XLA Ops:
  0.0 0.7 convert_bitcast_fusion
  0.7 1.4 %select_maximum_fusion.meta_ref = f32[8,128]{1,0:T(8,128)} fusion(f32[6,64]{1,0:T(8,128)} %bitcast.3, f32[6,64]{1,0:T(8,128)S(1)} %convert_bitcast_fusion), kind=kLoop, calls=%fused_computation | loop fusion | flops 5120 | bytes 7168 | tf_op jit(solution)/shard_map/concatenate | solution.py:419
  2.0 106.8 %moe.1 = bf16[64,2048]{1,0:T(8,128)(2,1)} custom-call(bf16[64,2048]{1,0:T(8,128)(2,1)} %x_ref.1, f32[8,128]{1,0:T(8,128)} %select_maximum_fusion.meta_ref, bf16[4,2048,1408]{2,1,0:T(8,128)(2,1)} %w1_ref.1, bf16[4,2048,1408]{2,1,0:T(8,128)(2,1)} %w3_ref.1, bf16[4,1408,2048]{2,1,0:T(8,128)(2,1)} %w2_ref.1), custom_call_target="tpu_custom_call" | custom-call | tf_op jit(solution)/shard_map/moe/pallas_call | solution.py:422
  108.9 1.7 %copy.8 = bf16[64,2048]{1,0:T(8,128)(2,1)} copy(bf16[64,2048]{1,0:T(8,128)(2,1)} %moe.1) | data formatting | bytes 524288
where the time goes:
time: 111 us
  Pallas kernels  107 us (96%)
  other arithmetic  2.04 us (2%)
  local copies, waits for them, and re-layouts  1.67 us (2%)
    pallas_call x1, Pallas kernels, local(): pl.pallas_call(functools.partial(_kernel, cfg), name='moe', out_shape=jax...  107 us

commit v1 on v0

--- a/solution.py
+++ b/solution.py
@@ -81,11 +81,8 @@
     x_copies = [pltpu.make_async_copy(x_ref.at[:, pl.ds(p * blk, blk)], xg.at[0, p, c], x_sem.at[p]) for p in range(NP)]
     m_copy = pltpu.make_async_copy(meta_ref, mg.at[0, c], m_sem)
     m_copy.start()
-    begin(x_copies)
-    for i in range(el - 1):
-        begin(w13_copies(i + 1, i))
-    for j in range(2):
-        begin(w2_copies(j, j))
+    for cp in x_copies:
+        cp.start()
 
     barrier = pltpu.get_barrier_semaphore()
     for dev in (right, left, partner):
@@ -134,16 +131,19 @@
     remote(mg.at[0, c], mg.at[0, c], mg_send, mgd_recv, partner).start()
     x_copies[0].wait()
     send(1, 0)
+    begin(w13_copies(1, 0))
+    meta_take(1)
     x_copies[1].wait()
+    send(1, 1)
     share(0, 0)
     share(0, 1)
     hc[...] = jnp.zeros(hc.shape, BF16)
-    meta_take(1)
-    send(1, 1)
     meta_take(2)
     take(1, 0)
+    begin(w13_copies(2, 1))
     meta_take(3)
     take(1, 1)
+    begin(w13_copies(3, 2))
     meta_take(4)
 
     def build():
@@ -200,6 +200,8 @@
     build()
     take(2, 0)
     take(2, 1)
+    for j in range(2):
+        begin(w2_copies(j, j))
 
     def dispatch(first, count, is_hot):
         start = count * rh

time: 111 us -> 102 us (0.919)
  Pallas kernels: 107 us -> 98.1 us
    pallas_call x1, Pallas kernels: 107 us -> 98.1 us  [local(): pl.pallas_call(functools.partial(_kernel, cfg), name='moe', out_shape=jax...]
where the time goes in v1:
time: 102 us
  Pallas kernels  98.1 us (96%)
  other arithmetic  2.04 us (2%)
  local copies, waits for them, and re-layouts  1.67 us (2%)
    pallas_call x1, Pallas kernels, local(): pl.pallas_call(functools.partial(_kernel, cfg), name='moe', out_shape=jax...  98.1 us

profile of v1, /device:TPU:30, one launch (start us, length us, event | category | flops | bytes accessed | tf_op | source)
XLA Modules:
  0.0 101.8 jit_solution(3148028293087612061)
XLA Ops:
  0.0 0.7 convert_bitcast_fusion
  0.7 1.4 %select_maximum_fusion.meta_ref = f32[8,128]{1,0:T(8,128)} fusion(f32[6,64]{1,0:T(8,128)} %bitcast.3, f32[6,64]{1,0:T(8,128)S(1)} %convert_bitcast_fusion), kind=kLoop, calls=%fused_computation | loop fusion | flops 5120 | bytes 7168 | tf_op jit(solution)/shard_map/concatenate | solution.py:421
  2.0 98.1 %moe.1 = bf16[64,2048]{1,0:T(8,128)(2,1)} custom-call(bf16[64,2048]{1,0:T(8,128)(2,1)} %x_ref.1, f32[8,128]{1,0:T(8,128)} %select_maximum_fusion.meta_ref, bf16[4,2048,1408]{2,1,0:T(8,128)(2,1)} %w1_ref.1, bf16[4,2048,1408]{2,1,0:T(8,128)(2,1)} %w3_ref.1, bf16[4,1408,2048]{2,1,0:T(8,128)(2,1)} %w2_ref.1), custom_call_target="tpu_custom_call" | custom-call | tf_op jit(solution)/shard_map/moe/pallas_call | solution.py:424
  100.1 1.7 %copy.8 = bf16[64,2048]{1,0:T(8,128)(2,1)} copy(bf16[64,2048]{1,0:T(8,128)(2,1)} %moe.1) | data formatting | bytes 524288
